TPU v7x, 32 devices: a whole 2x2x4 slice. The times are simulated.
32 devices in a mesh: rep: 4 (over y, x), fsdp: 4 (over z), tp: 2 (over core).
Axes of the slice: x: 2, y: 2, z: 4, core: 2. Of those that a mesh axis runs over, the one named last changes fastest.
Arguments:
- hidden: bfloat16 [4096, 4096], P(('rep', 'fsdp')), may hold values from -6 to 6
- norm_gain: float32 [4096], P('fsdp'), may hold values from 0.5 to 1.5
- value_weight: bfloat16 [4096, 1024], P('fsdp', 'tp'), may hold values from -0.09375 to 0.09375
- value_grad: bfloat16 [4096, 1024], P(('rep', 'fsdp'), 'tp'), may hold values from -6 to 6
Outputs:
- input_grad: bfloat16 [4096, 4096], P(('rep', 'fsdp'))
- weight_grad: float32 [4096, 1024], P('fsdp', 'tp')
- gain_grad: float32 [4096], P('fsdp')
All inputs are finite; a program needn't handle non-finite values.
Results may differ from a plain program's by a relative error of at most 0.00125.
Values may be sent and summed in bfloat16 or wider, within the bound.
A program may use at most 64 MiB of HBM per device.

v0:
```python
import jax
import jax.numpy as jnp
from jax import lax
from jax.sharding import PartitionSpec as P

D = 4096


epsilon = 1e-05


def shards(hidden, norm_gain, value_weight, value_grad):
    average = 1.0 / (lax.axis_size("rep") * lax.axis_size("fsdp"))
    inputs = hidden.astype(jnp.float32)
    inv_local = lax.rsqrt(jnp.mean(inputs * inputs, axis=1, keepdims=True) + epsilon)
    columns = lax.all_to_all(hidden, "fsdp", split_axis=1, concat_axis=0, tiled=True)
    inv_rms = lax.all_gather(inv_local, "fsdp", axis=0, tiled=True)
    normal = columns.astype(jnp.float32) * inv_rms
    normed = (normal * norm_gain).astype(jnp.bfloat16)
    group_grad = lax.all_gather(value_grad, "fsdp", axis=0, tiled=True)
    partial_grad = jnp.dot(group_grad, value_weight.T, preferred_element_type=jnp.float32)
    grad_normed = lax.psum(partial_grad, "tp")
    weight_part = jnp.dot(normed.T, group_grad, preferred_element_type=jnp.float32)
    gain_part = jnp.sum(grad_normed * normal, axis=0)
    grad_scaled = grad_normed * norm_gain
    row_total = lax.psum(
        jnp.sum(grad_scaled * normal, axis=1, keepdims=True).astype(jnp.bfloat16), "fsdp"
    ).astype(jnp.float32)
    center = row_total / D
    column_grad = (inv_rms * (grad_scaled - normal * center)).astype(jnp.bfloat16)
    input_grad = lax.all_to_all(column_grad, "fsdp", split_axis=0, concat_axis=1, tiled=True)
    weight_total = lax.psum(weight_part, "rep")
    gain_total = lax.psum(gain_part, "rep")
    return (input_grad, weight_total * average, gain_total * average)


def solution(mesh):
    placed = (P(("rep", "fsdp"), None), P("fsdp"), P("fsdp", "tp"), P(("rep", "fsdp"), "tp"))
    return jax.shard_map(
        shards,
        mesh=mesh,
        in_specs=placed,
        out_specs=(P(("rep", "fsdp"), None), P("fsdp", "tp"), P("fsdp")),
        check_vma=False,
    )
```

profile of v0, /device:TPU:0, one launch (start us, length us, event | category | flops | bytes accessed | tf_op | source)
XLA Modules:
  0.0 209.0 jit_solution(1176009656137438168)
XLA Ops:
  7.2 0.0 copy-start
  7.2 0.0 all-gather.4.cloned.1.call-start
  7.2 0.7 all-gather.4.cloned.1.call-update
  7.9 0.0 all-reduce.3.cloned.1.call-start
  8.0 32.4 %all-gather.4.cloned.1.call-done = bf16[1024,512]{1,0:T(8,128)(2,1)} async-done(((bf16[256,512]{1,0:T(8,128)(2,1)}), bf16[1024,512]{1,0:T(8,128)(2,1)}) %all-gather.4.cloned.1.call-update) | async-done | bytes 1048592 | tf_op jit(solution)/shard_map/all_gather | solution.py:20
  40.3 0.0 copy-done
  40.3 4.5 %fusion = f32[1024,1024]{1,0:T(8,128)} fusion(bf16[1024,512]{1,0:T(8,128)(2,1)} %all-gather.4.cloned.1.call-done, bf16[1024,512]{1,0:T(8,128)(2,1)S(1)} %copy-done), kind=kOutput, calls=%fused_computation.11 | convolution fusion | flops 1073741824 | bytes 6291456 | tf_op jit(solution)/shard_map/dot_general | solution.py:21
  44.8 0.0 copy-start.1
  44.8 0.0 all-reduce.3.cloned.1.call-update
  44.9 1.6 copy-done.1
  46.4 1.5 copy.16
  48.0 0.0 copy-start.2
  48.0 3.7 %all-to-all-start = ((bf16[256,4,1024]{2,0,1:T(8,128)(2,1)}), bf16[256,4,1024]{2,0,1:T(8,128)(2,1)S(1)}, u32[]{:S(2)}, u32[]{:S(2)}) async-start(bf16[256,4,1024]{2,0,1:T(8,128)(2,1)} %bitcast.29), calls=%async_computation | async-start | bytes 4194304 | tf_op jit(solution)/shard_map/all_to_all | solution.py:16
  51.7 2.1 multiply_reduce_fusion.2
  53.8 37.2 %all-gather.1 = f32[4,1,256]{2,1,0:T(1,128)S(1)} all-gather(f32[1,1,256]{2,1,0:T(1,128)S(1)} %bitcast.35), channel_id=2, replica_groups=mesh['rep'=4,'fsdp'=4,'tp'=2] {'fsdp'}, dimensions={0}, use_global_device_ids=true | all-gather | bytes 5120 | tf_op jit(solution)/shard_map/all_gather | solution.py:17
  91.0 8.2 %all-to-all-done = bf16[256,4,1024]{2,0,1:T(8,128)(2,1)S(1)} async-done(((bf16[256,4,1024]{2,0,1:T(8,128)(2,1)}), bf16[256,4,1024]{2,0,1:T(8,128)(2,1)S(1)}, u32[]{:S(2)}, u32[]{:S(2)}) %all-to-all-start) | async-done | bytes 2097184 | tf_op jit(solution)/shard_map/all_to_all | solution.py:16
  99.3 0.0 all-reduce.3.cloned.1.call-done
  99.3 0.0 copy-done.2
  99.3 3.3 %multiply_reduce_fusion = (f32[1024]{0:T(1024)S(1)}, bf16[1024]{0:T(1024)(128)(2,1)S(1)}) fusion(f32[1024,1024]{1,0:T(8,128)} %all-reduce.3.cloned.1.call-done, bf16[256,4,1024]{2,0,1:T(8,128)(2,1)S(1)} %all-to-all-done, f32[1024]{0:T(1024)S(1)} %bitcast.32, f32[1024]{0:T(1024)S(1)} %copy-done.2), kind=kLoop, calls=%fused_computation.1 | loop fusion | flops 7337984 | bytes 6305792 | tf_op jit(solution)/shard_map/reduce_sum | solution.py:24
  102.6 12.0 %psum.29 = bf16[1024,1]{0,1:T(2,128)(2,1)S(1)} all-reduce(bf16[1024,1]{0,1:T(2,128)(2,1)S(1)} %convert_element_type.40), channel_id=1, replica_groups=mesh['rep'=4,'fsdp'=4,'tp'=2] {'fsdp'}, use_global_device_ids=true, to_apply=%region_3.0 | all-reduce | flops 1024 | bytes 4096 | tf_op jit(solution)/shard_map/psum | solution.py:26
  114.7 4.3 %multiply_convert_fusion = (bf16[1024,1024]{1,0:T(8,128)(2,1)}, bf16[1024,1024]{1,0:T(8,128)(2,1)}) fusion(bf16[256,4,1024]{2,0,1:T(8,128)(2,1)S(1)} %all-to-all-done, f32[1024]{0:T(1024)S(1)} %bitcast.33, f32[1024]{0:T(1024)S(1)} %copy-done.2, f32[1024]{0:T(1024)S(1)} %bitcast.34, f32[1024,1024]{1,0:T(8,128)} %all-reduce.3.cloned.1.call-done), kind=kLoop, calls=%fused_computation.2 | loop fusion | flops 9437184 | bytes 10498048 | tf_op jit(solution)/shard_map/convert_element_type | solution.py:19
  118.9 3.6 %all-to-all-start.1 = ((bf16[4,256,1024]{2,1,0:T(8,128)(2,1)}), bf16[4,256,1024]{2,1,0:T(8,128)(2,1)S(1)}, u32[]{:S(2)}, u32[]{:S(2)}) async-start(bf16[4,256,1024]{2,1,0:T(8,128)(2,1)} %bitcast.30), calls=%async_computation.1 | async-start | bytes 4194304 | tf_op jit(solution)/shard_map/all_to_all | solution.py:31
  122.6 0.0 all-reduce.5.cloned.1.call-start
  122.6 4.5 %fusion.1 = f32[1024,512]{1,0:T(8,128)} fusion(bf16[1024,1024]{1,0:T(8,128)(2,1)} %get-tuple-element.5, bf16[1024,512]{1,0:T(8,128)(2,1)} %all-gather.4.cloned.1.call-done), kind=kOutput, calls=%fused_computation.12 | convolution fusion | flops 1073741824 | bytes 5242880 | tf_op jit(solution)/shard_map/dot_general | solution.py:23
  127.1 0.0 all-reduce.5.cloned.1.call-update
  127.1 9.9 %psum.31 = f32[1024]{0:T(1024)S(1)} all-reduce(f32[1024]{0:T(1024)S(1)} %get-tuple-element.3), channel_id=1, replica_groups=mesh['rep'=4,'fsdp'=4,'tp'=2] {'rep'}, use_global_device_ids=true, to_apply=%region_6.0 | all-reduce | flops 1024 | bytes 8192 | tf_op jit(solution)/shard_map/psum | solution.py:33
  137.1 0.6 broadcast_multiply_fusion.1
  137.7 60.1 %all-reduce.5.cloned.1.call-done = f32[1024,512]{1,0:T(8,128)} async-done(((f32[1024,512]{1,0:T(8,128)}), f32[1024,512]{1,0:T(8,128)}) %all-reduce.5.cloned.1.call-update) | async-done | bytes 2097168 | tf_op jit(solution)/shard_map/psum | solution.py:32
  197.7 3.1 %broadcast_multiply_fusion = f32[1024,512]{1,0:T(8,128)} fusion(f32[1024,512]{1,0:T(8,128)} %all-reduce.5.cloned.1.call-done), kind=kLoop, calls=%fused_computation.7 | loop fusion | flops 524288 | bytes 4194304 | tf_op jit(solution)/shard_map/mul | solution.py:34
  200.9 0.0 all-to-all-done.1
  200.9 1.6 copy.14
  (3 shorter events, 0.0 us)
Async XLA Ops:
  7.2 33.2 %copy-start = (bf16[1024,512]{1,0:T(8,128)(2,1)S(1)}, bf16[1024,512]{1,0:T(8,128)(2,1)}, u32[]{:S(2)}) copy-start(bf16[1024,512]{1,0:T(8,128)(2,1)} %param.6) | copy-start | bytes 3145732
  7.2 33.2 %all-gather.4.cloned.1.call-start = ((), (), s32[]{:S(2)}) async-start(), calls=%async_computation.2 | async-start | bytes 1310720 | tf_op jit(solution)/shard_map/all_gather | solution.py:20
  7.9 91.3 %all-reduce.3.cloned.1.call-start = ((), (), s32[]{:S(2)}) async-start(), calls=%async_computation.3 | async-start | bytes 8388608 | tf_op jit(solution)/shard_map/psum | solution.py:22
  44.8 1.6 copy-start.1
  48.0 51.3 %copy-start.2 = (f32[1024]{0:T(1024)S(1)}, f32[1024]{0:T(1024)}, u32[]{:S(2)}) copy-start(f32[1024]{0:T(1024)} %param.5) | copy-start | bytes 12292
  48.0 51.3 %all-to-all-start = ((bf16[256,4,1024]{2,0,1:T(8,128)(2,1)}), bf16[256,4,1024]{2,0,1:T(8,128)(2,1)S(1)}, u32[]{:S(2)}, u32[]{:S(2)}) async-start(bf16[256,4,1024]{2,0,1:T(8,128)(2,1)} %bitcast.29), calls=%async_computation | async-start | bytes 4194304 | tf_op jit(solution)/shard_map/all_to_all | solution.py:16
  118.9 81.9 %all-to-all-start.1 = ((bf16[4,256,1024]{2,1,0:T(8,128)(2,1)}), bf16[4,256,1024]{2,1,0:T(8,128)(2,1)S(1)}, u32[]{:S(2)}, u32[]{:S(2)}) async-start(bf16[4,256,1024]{2,1,0:T(8,128)(2,1)} %bitcast.30), calls=%async_computation.1 | async-start | bytes 4194304 | tf_op jit(solution)/shard_map/all_to_all | solution.py:31
  122.6 75.2 %all-reduce.5.cloned.1.call-start = ((), (), s32[]{:S(2)}) async-start(), calls=%async_computation.4 | async-start | bytes 4194304 | tf_op jit(solution)/shard_map/psum | solution.py:32
Sparse Core Ops, SparseCore 0:
  9.6 30.7 all-gather.3
  45.0 27.4 all-reduce.2
  127.2 70.4 all-reduce.4
where the time goes:
time: 210 us; the launch traced here: 209 us
  waiting for transfers between devices  101 us (48%)
  blocking collectives  59.2 us (28%)
  between operations  13.8 us (7%)
  other arithmetic  13.5 us (6%)
  matrix products  8.97 us (4%)
  starting transfers between devices  7.47 us (4%)
  local copies, waits for them, and re-layouts  4.69 us (2%)
    psum x1, waiting for transfers between devices, shards(): weight_total = lax.psum(weight_part, 'rep')  60.1 us
    all_gather x1, blocking collectives, shards(): inv_rms = lax.all_gather(inv_local, 'fsdp', axis=0, tiled=True)  37.2 us
    all_gather x1, waiting for transfers between devices, shards(): group_grad = lax.all_gather(value_grad, 'fsdp', axis=0, tiled=True)  32.4 us
    psum x1, blocking collectives, shards(): lax.psum(jnp.sum(grad_scaled * normal, axis=1, keepdims=True).astype(jnp....  12 us
    psum x1, blocking collectives, shards(): gain_total = lax.psum(gain_part, 'rep')  9.94 us
    all_to_all x1, waiting for transfers between devices, shards(): lax.all_to_all(hidden, 'fsdp', split_axis=1, concat_axis=0, tiled=True)  8.22 us
    dot_general x1, matrix products, shards(): jnp.dot(normed.T, group_grad, preferred_element_type=jnp.float32)  4.5 us
    dot_general x1, matrix products, shards(): jnp.dot(group_grad, value_weight.T, preferred_element_type=jnp.float32)  4.48 us
  transfers between devices with their start and end apart: 5, of which 3 were waited for; matrix products, arithmetic and copies ran while one was open for 6% of the time, Pallas kernels for 0%

commit v1 on v0

v1 whole, which is shorter than its diff:
```python
import functools

import jax
import jax.numpy as jnp
from jax import lax
from jax.experimental import pallas as pl
from jax.experimental.pallas import tpu as pltpu
from jax.sharding import PartitionSpec as P

epsilon = 1e-05
MESH = pl.DeviceIdType.MESH
ROWS = 32
LANES = 128


def kernel(sizes, hid, gain, w, vg, dx, dw, dgain,
           hv, cols, nm, vgs, vgx, wx, invc, inv_rows, gn, rsc, rs, cenc, cg, wp, wr, gacc, gbuf,
           s_load, s_h, r_h, s_hx, r_hx, s_v, r_v, s_vx, r_vx, s_w, r_w, s_i, r_i,
           s_rs, r_rs, s_b, r_b, s_bx, r_bx, s_p, r_p, s_q, r_q, s_g, r_g):
    nrep, n, ntp = sizes
    r, f, c = lax.axis_index("rep"), lax.axis_index("fsdp"), lax.axis_index("tp")
    T, D = hid.shape
    F, K = w.shape
    Th = T // ntp
    Fq = F // nrep
    average = 1.0 / (nrep * n)
    wide = F // LANES

    def remote(src, dst, ssem, rsem, dev):
        return pltpu.make_async_remote_copy(src_ref=src, dst_ref=dst, send_sem=ssem, recv_sem=rsem,
                                            device_id=dev, device_id_type=MESH)

    def half(j, h):
        return pl.ds(pl.multiple_of(j * T + h * Th, LANES), Th)

    def full(j):
        return pl.ds(pl.multiple_of(j * T, LANES), T)

    def feats(j):
        return pl.ds(pl.multiple_of(j * F, LANES), F)

    def tokens(h):
        return pl.ds(pl.multiple_of(h * Th, LANES), Th)

    zpeer = [lax.rem(f + s, n) for s in range(n)]
    tpeer = [lax.rem(c + s, ntp) for s in range(ntp)]
    rpeer = [lax.rem(r + s, nrep) for s in range(nrep)]
    zfrom = [lax.rem(f + n - s, n) for s in range(n)]

    load_h = pltpu.make_async_copy(hid, hv, s_load.at[0])
    load_v = pltpu.make_async_copy(vg, vgs.at[full(f)], s_load.at[1])
    load_w = pltpu.make_async_copy(w, wx.at[c], s_load.at[2])
    load_h.start()
    load_v.start()
    load_w.start()

    barrier = pltpu.get_barrier_semaphore()
    for s in range(1, n):
        pl.semaphore_signal(barrier, inc=1, device_id={"fsdp": zpeer[s]}, device_id_type=MESH)
    for a in range(nrep):
        for b in range(ntp):
            if a or b:
                pl.semaphore_signal(barrier, inc=1, device_id={"rep": rpeer[a], "tp": tpeer[b]}, device_id_type=MESH)
    pl.semaphore_wait(barrier, n - 1 + nrep * ntp - 1)

    def send_v(s):
        return remote(vg, vgs.at[full(f)], s_v.at[s], r_v.at[s], {"fsdp": zpeer[s]})

    def got_v(s):
        return remote(vg, vgs.at[full(zfrom[s])], s_v.at[s], r_v.at[s], {"fsdp": zpeer[s]})

    def send_h(s):
        return remote(hid.at[tokens(c), feats(zpeer[s])], cols.at[half(f, c)], s_h.at[s], r_h.at[s], {"fsdp": zpeer[s]})

    def got_h(s):
        return remote(hid.at[tokens(c), feats(f)], cols.at[half(zfrom[s], c)], s_h.at[s], r_h.at[s], {"fsdp": zpeer[s]})

    def send_i(s):
        return remote(inv_rows.at[f], inv_rows.at[f], s_i.at[s], r_i.at[s], {"fsdp": zpeer[s]})

    def got_i(s):
        return remote(inv_rows.at[f], inv_rows.at[zfrom[s]], s_i.at[s], r_i.at[s], {"fsdp": zpeer[s]})

    def pass_v(s, b):
        j = zfrom[s]
        src = vg.at[tokens(tpeer[b])] if s == 0 else vgs.at[half(j, tpeer[b])]
        return remote(src, vgx.at[b, pl.ds(pl.multiple_of(j * Th, LANES), Th)],
                      s_vx.at[b, s], r_vx.at[b, s], {"tp": tpeer[b]})

    def pass_h(s, b):
        rows = half(zfrom[s], c)
        return remote(cols.at[rows], cols.at[rows], s_hx.at[b, s], r_hx.at[b, s], {"tp": tpeer[b]})

    def took_h(s, b):
        rows = half(zfrom[s], lax.rem(c + ntp - b, ntp))
        return remote(cols.at[rows], cols.at[rows], s_hx.at[b, s], r_hx.at[b, s], {"tp": tpeer[b]})

    def pass_w(b):
        return remote(w, wx.at[c], s_w.at[b], r_w.at[b], {"tp": tpeer[b]})

    def took_w(b):
        return remote(w, wx.at[lax.rem(c + ntp - b, ntp)], s_w.at[b], r_w.at[b], {"tp": tpeer[b]})

    for s in range(1, n):
        send_v(s).start()
    for s in range(1, n):
        send_h(s).start()
    for b in range(1, ntp):
        pass_w(b).start()
        pass_v(0, b).start()

    load_h.wait()

    @pl.loop(0, T // ROWS)
    def _(i):
        rows = pl.ds(pl.multiple_of(i * ROWS, ROWS), ROWS)
        acc = jnp.zeros((ROWS, LANES), jnp.float32)
        for k in range(D // LANES):
            x = hv[rows, k * LANES:(k + 1) * LANES].astype(jnp.float32)
            acc = acc + x * x
        inv = lax.rsqrt(jnp.sum(acc, axis=1, keepdims=True) / D + epsilon)
        invc[pl.ds(pl.multiple_of(f * T + i * ROWS, ROWS), ROWS), :] = jnp.broadcast_to(inv, (ROWS, LANES))

    for k in range(T // LANES):
        block = invc[pl.ds(pl.multiple_of(f * T + k * LANES, LANES), LANES), :]
        inv_rows[f, :, k * LANES:(k + 1) * LANES] = block.T[:8, :]
    for s in range(1, n):
        send_i(s).start()
    cols[full(f), :] = hv[:, feats(f)]

    def spread(x):
        return jnp.concatenate([x] * wide, axis=1) if wide > 1 else x

    gains = gain[...]

    def normalise(first, count):
        @pl.loop(0, count // ROWS)
        def _(i):
            rows = pl.ds(pl.multiple_of(first + i * ROWS, ROWS), ROWS)
            normal = cols[rows, :].astype(jnp.float32) * spread(invc[rows, :])
            nm[rows, :] = (normal * gains).astype(jnp.bfloat16)

    normalise(f * T, T)
    load_v.wait()
    load_w.wait()
    for b in range(1, ntp):
        took_w(b).wait_recv()
        pass_v(0, b).wait_recv()
    gacc[...] = jnp.zeros_like(gacc)

    def products(j):
        vrows = pl.ds(pl.multiple_of(j * Th, LANES), Th)
        total = lax.dot_general(vgs[half(j, c), :], wx[c], (((1,), (1,)), ((), ())), preferred_element_type=jnp.float32)
        for b in range(1, ntp):
            total = total + lax.dot_general(vgx[b, vrows, :], wx[lax.rem(c + ntp - b, ntp)], (((1,), (1,)), ((), ())),
                                            preferred_element_type=jnp.float32)
        gn[vrows, :] = total

        @pl.loop(0, Th // ROWS)
        def _(i):
            rows = pl.ds(pl.multiple_of(j * T + c * Th + i * ROWS, ROWS), ROWS)
            mine = pl.ds(pl.multiple_of(j * Th + i * ROWS, ROWS), ROWS)
            normal = cols[rows, :].astype(jnp.float32) * spread(invc[rows, :])
            t = gn[mine, :] * normal
            gacc[...] += jnp.sum(t.reshape(ROWS // 8, 8, F), axis=0)
            rsc[pl.ds(pl.multiple_of(i * ROWS, ROWS), ROWS), :] = jnp.broadcast_to(
                jnp.sum(t * gains, axis=1, keepdims=True), (ROWS, LANES))

        for k in range(Th // LANES):
            rs[f, pl.ds(j, 1), k * LANES:(k + 1) * LANES] = rsc[k * LANES:(k + 1) * LANES, :].T[:1, :]

    products(f)
    for s in range(1, n):
        got_v(s).wait_recv()
        for b in range(1, ntp):
            pass_v(s, b).start()
    for s in range(1, n):
        j = zfrom[s]
        got_h(s).wait_recv()
        for b in range(1, ntp):
            pass_h(s, b).start()
        got_i(s).wait_recv()
        for k in range(T // LANES):
            row = inv_rows[j, :1, k * LANES:(k + 1) * LANES]
            invc[pl.ds(pl.multiple_of(j * T + k * LANES, LANES), LANES), :] = jnp.broadcast_to(row, (LANES, LANES)).T
        for b in range(1, ntp):
            pass_v(s, b).wait_recv()
            took_h(s, b).wait_recv()
        normalise(j * T, T)

    def quarter(q):
        return pl.ds(pl.multiple_of(q * Fq, 8), Fq)

    def send_p(s):
        return remote(wp.at[quarter(rpeer[s])], wr.at[s], s_p.at[s], r_p.at[s], {"rep": rpeer[s]})

    def partial_of(columns):
        return lax.dot_general(nm[:, columns], vgs[...], (((0,), (0,)), ((), ())), preferred_element_type=jnp.float32)

    if Fq % LANES == 0:
        for s in [*range(1, nrep), 0]:
            q = rpeer[s]
            wp[quarter(q), :] = partial_of(pl.ds(pl.multiple_of(q * Fq, LANES), Fq))
            if s:
                send_p(s).start()
    else:
        wp[...] = partial_of(slice(None))
        for s in range(1, nrep):
            send_p(s).start()

    for s in range(1, n):
        products(zfrom[s])

    def send_rs(s):
        return remote(rs.at[f], rs.at[f], s_rs.at[s], r_rs.at[s], {"fsdp": zpeer[s]})

    def got_rs(s):
        return remote(rs.at[f], rs.at[zfrom[s]], s_rs.at[s], r_rs.at[s], {"fsdp": zpeer[s]})

    for s in range(1, n):
        send_rs(s).start()

    slot = r * ntp + c
    gbuf[slot] = jnp.sum(gacc[...], axis=0, keepdims=True)

    def send_g(a, b):
        return remote(gbuf.at[slot], gbuf.at[slot], s_g.at[a, b], r_g.at[a, b], {"rep": rpeer[a], "tp": tpeer[b]})

    def got_g(a, b):
        src = lax.rem(r + nrep - a, nrep) * ntp + lax.rem(c + ntp - b, ntp)
        return remote(gbuf.at[slot], gbuf.at[src], s_g.at[a, b], r_g.at[a, b], {"rep": rpeer[a], "tp": tpeer[b]})

    others = [(a, b) for a in range(nrep) for b in range(ntp) if a or b]
    for a, b in others:
        send_g(a, b).start()

    for s in range(1, n):
        got_rs(s).wait_recv()
    center = rs[0]
    for s in range(1, n):
        center = center + rs[s]
    rs_total = center / D
    rsc_rows = rs_total.shape[0]

    def send_b(s):
        return remote(cg.at[pl.ds(pl.multiple_of(zpeer[s] * Th, LANES), Th)], dx.at[tokens(c), feats(f)],
                      s_b.at[s], r_b.at[s], {"fsdp": zpeer[s]})

    def got_b(s):
        return remote(cg.at[pl.ds(0, Th)], dx.at[tokens(c), feats(zfrom[s])],
                      s_b.at[s], r_b.at[s], {"fsdp": zpeer[s]})

    def pass_b(s, b):
        ref = dx.at[tokens(c), feats(zfrom[s])]
        return remote(ref, ref, s_bx.at[b, s], r_bx.at[b, s], {"tp": tpeer[b]})

    def took_b(s, b):
        ref = dx.at[tokens(lax.rem(c + ntp - b, ntp)), feats(zfrom[s])]
        return remote(ref, ref, s_bx.at[b, s], r_bx.at[b, s], {"tp": tpeer[b]})

    cenc[...] = rs_total
    for s in [*range(1, n), 0]:
        j = zpeer[s]
        for k in range(Th // LANES):
            row = cenc[pl.ds(j, 1), k * LANES:(k + 1) * LANES]
            rsc[k * LANES:(k + 1) * LANES, :] = jnp.broadcast_to(row, (LANES, LANES)).T

        @pl.loop(0, Th // ROWS)
        def _(i):
            rows = pl.ds(pl.multiple_of(j * T + c * Th + i * ROWS, ROWS), ROWS)
            mine = pl.ds(pl.multiple_of(j * Th + i * ROWS, ROWS), ROWS)
            inv = spread(invc[rows, :])
            normal = cols[rows, :].astype(jnp.float32) * inv
            cen = spread(rsc[pl.ds(pl.multiple_of(i * ROWS, ROWS), ROWS), :])
            cg[mine, :] = (inv * (gn[mine, :] * gains - normal * cen)).astype(jnp.bfloat16)

        if s:
            send_b(s).start()
        else:
            dx[tokens(c), feats(f)] = cg[pl.ds(pl.multiple_of(f * Th, LANES), Th), :]
            for b in range(1, ntp):
                pass_b(0, b).start()

    def send_q(s):
        return remote(dw.at[quarter(r)], dw.at[quarter(r)], s_q.at[s], r_q.at[s], {"rep": rpeer[s]})

    def got_q(s):
        ref = dw.at[quarter(lax.rem(r + nrep - s, nrep))]
        return remote(ref, ref, s_q.at[s], r_q.at[s], {"rep": rpeer[s]})

    for s in range(1, nrep):
        send_p(s).wait_recv()
    total = wp[quarter(r), :]
    for s in range(1, nrep):
        total = total + wr[s]
    dw[quarter(r), :] = total * average
    for s in range(1, nrep):
        send_q(s).start()

    for a, b in others:
        got_g(a, b).wait_recv()
    gsum = gbuf[0]
    for i in range(1, nrep * ntp):
        gsum = gsum + gbuf[i]
    dgain[...] = gsum * average

    for s in range(1, n):
        got_b(s).wait_recv()
        for b in range(1, ntp):
            pass_b(s, b).start()
    for s in range(1, nrep):
        got_q(s).wait_recv()
    for s in range(n):
        for b in range(1, ntp):
            took_b(s, b).wait_recv()
    for s in range(1, n):
        for copy in (send_v(s), send_h(s), send_i(s), send_rs(s), send_b(s)):
            copy.wait_send()
    for s in range(1, nrep):
        send_p(s).wait_send()
        send_q(s).wait_send()
    for a, b in others:
        send_g(a, b).wait_send()
    for b in range(1, ntp):
        pass_w(b).wait_send()
        for s in range(n):
            pass_v(s, b).wait_send()
            pass_b(s, b).wait_send()
            if s:
                pass_h(s, b).wait_send()


def shards(hidden, norm_gain, value_weight, value_grad):
    nrep, n, ntp = (lax.axis_size(a) for a in ("rep", "fsdp", "tp"))
    T, D = hidden.shape
    F, K = value_weight.shape
    Th, Fq = T // ntp, F // nrep
    G = n * T
    n8 = -(-n // 8) * 8
    dma = pltpu.SemaphoreType.DMA
    f32, bf16 = jnp.float32, jnp.bfloat16
    V = pltpu.VMEM
    vmem = pl.BlockSpec(memory_space=pltpu.VMEM)
    hbm = pl.BlockSpec(memory_space=pl.ANY)
    dx, dw, dgain = pl.pallas_call(
        functools.partial(kernel, (nrep, n, ntp)),
        out_shape=(jax.ShapeDtypeStruct((T, D), bf16), jax.ShapeDtypeStruct((F, K), f32),
                   jax.ShapeDtypeStruct((1, F), f32)),
        in_specs=[hbm, vmem, hbm, hbm],
        out_specs=(vmem, vmem, vmem),
        scratch_shapes=[
            V((T, D), bf16), V((G, F), bf16), V((G, F), bf16), V((G, K), bf16), V((ntp, n * Th, K), bf16),
            V((ntp, F, K), bf16), V((G, LANES), f32), V((n, 8, T), f32), V((n * Th, F), f32), V((Th, LANES), f32),
            V((n, n8, Th), f32), V((n8, Th), f32), V((n * Th, F), bf16), V((F, K), f32), V((nrep, Fq, K), f32),
            V((8, F), f32), V((nrep * ntp, 1, F), f32),
            dma((3,)), dma((n,)), dma((n,)), dma((ntp, n)), dma((ntp, n)), dma((n,)), dma((n,)),
            dma((ntp, n)), dma((ntp, n)), dma((ntp,)), dma((ntp,)), dma((n,)), dma((n,)),
            dma((n,)), dma((n,)), dma((n,)), dma((n,)), dma((ntp, n)), dma((ntp, n)),
            dma((nrep,)), dma((nrep,)), dma((nrep,)), dma((nrep,)), dma((nrep, ntp)), dma((nrep, ntp)),
        ],
        compiler_params=pltpu.CompilerParams(collective_id=0, has_side_effects=True, vmem_limit_bytes=60 * 1024 * 1024),
    )(hidden, norm_gain.reshape(1, F), value_weight, value_grad)
    return dx, dw, dgain.reshape(F)


def solution(mesh):
    placed = (P(("rep", "fsdp"), None), P("fsdp"), P("fsdp", "tp"), P(("rep", "fsdp"), "tp"))
    return jax.shard_map(
        shards,
        mesh=mesh,
        in_specs=placed,
        out_specs=(P(("rep", "fsdp"), None), P("fsdp", "tp"), P("fsdp")),
        check_vma=False,
    )
```

time: 210 us -> 114 us (0.54)
  Pallas kernels: 0 us -> 108 us
  waiting for transfers between devices: 101 us -> 0 us
  blocking collectives: 59.2 us -> 0 us
  other arithmetic: 13.5 us -> 0 us
  between operations: 13.8 us -> 0.65 us
  matrix products: 8.97 us -> 0 us
  starting transfers between devices: 7.47 us -> 0 us
    pallas_call x0 -> x1, Pallas kernels: none -> 108 us  [shards(): pl.pallas_call(functools.partial(kernel, (nrep, n, ntp)), out_shape=(jax....]
    psum x2 -> x0, waiting for transfers between devices: 60.1 us -> none  [the longest x1 60.1 us: shards(): weight_total = lax.psum(weight_part, 'rep')]
    all_gather x1 -> x0, blocking collectives: 37.2 us -> none  [shards(): inv_rms = lax.all_gather(inv_local, 'fsdp', axis=0, tiled=True)]
    all_gather x1 -> x0, waiting for transfers between devices: 32.4 us -> none  [shards(): group_grad = lax.all_gather(value_grad, 'fsdp', axis=0, tiled=True)]
    psum x2 -> x0, blocking collectives: 22 us -> none  [the longest x1 12 us: shards(): lax.psum(jnp.sum(grad_scaled * normal, axis=1, keepdims=True).astype(jnp....]
    dot_general x2 -> x0, matrix products: 8.97 us -> none  [the longest x1 4.5 us: shards(): jnp.dot(normed.T, group_grad, preferred_element_type=jnp.float32)]
    all_to_all x2 -> x0, waiting for transfers between devices: 8.22 us -> none  [the longest x1 8.22 us: shards(): lax.all_to_all(hidden, 'fsdp', split_axis=1, concat_axis=0, tiled=True)]
    all_to_all x2 -> x0, starting transfers between devices: 7.35 us -> none  [the longest x1 3.74 us: shards(): lax.all_to_all(hidden, 'fsdp', split_axis=1, concat_axis=0, tiled=True)]
  transfers between devices with their start and end apart: 5 -> 0, of which waited for: 3 -> 0; matrix products, arithmetic and copies ran while one was open for 6% -> 0% of each run, Pallas kernels for 0% -> 0%
where the time goes in v1:
time: 114 us
  Pallas kernels  108 us (95%)
  local copies, waits for them, and re-layouts  5.2 us (5%)
    pallas_call x1, Pallas kernels, shards(): pl.pallas_call(functools.partial(kernel, (nrep, n, ntp)), out_shape=(jax....  108 us
    unnamed x7, local copies, waits for them, and re-layouts  5.2 us

profile of v1, /device:TPU:0, one launch (start us, length us, event | category | flops | bytes accessed | tf_op | source)
XLA Modules:
  0.0 113.5 jit_solution(9325282714224095744)
XLA Ops:
  0.6 107.7 %shard_map.67 = (bf16[256,4096]{1,0:T(8,128)(2,1)}, f32[1024,512]{1,0:T(8,128)}, f32[1,1024]{1,0:T(1,128)}) custom-call(bf16[256,4096]{1,0:T(8,128)(2,1)} %hid.1, f32[1,1024]{1,0:T(1,128)} %bitcast.2, bf16[1024,512]{1,0:T(8,128)(2,1)} %w.1, bf16[256,512]{1,0:T(8,128)(2,1)} %vg.1), custom_call_target="tpu_custom_call" | custom-call | tf_op jit(solution)/shard_map/pallas_call | solution.py:345
  108.3 0.0 copy-start
  108.3 3.3 %copy.10 = bf16[256,4096]{1,0:T(8,128)(2,1)} copy(bf16[256,4096]{1,0:T(8,128)(2,1)} %get-tuple-element.12) | data formatting | bytes 4194304
  111.6 0.0 copy-done
  111.6 0.0 copy-start.1
  111.6 1.3 %copy.11 = f32[1024,512]{1,0:T(8,128)} copy(f32[1024,512]{1,0:T(8,128)S(1)} %copy-done) | data formatting | bytes 4194304
  112.9 0.0 copy-done.1
  112.9 0.6 copy.12
Async XLA Ops:
  108.3 3.3 %copy-start = (f32[1024,512]{1,0:T(8,128)S(1)}, f32[1024,512]{1,0:T(8,128)}, u32[]{:S(2)}) copy-start(f32[1024,512]{1,0:T(8,128)} %get-tuple-element.13) | copy-start | bytes 6291460
  111.6 1.3 %copy-start.1 = (f32[1,1024]{1,0:T(1,128)S(1)}, f32[1,1024]{1,0:T(1,128)}, u32[]{:S(2)}) copy-start(f32[1,1024]{1,0:T(1,128)} %get-tuple-element.8) | copy-start | bytes 12292

commit v2 on v1

v2 whole, which is shorter than its diff:
```python
import functools

import jax
import jax.numpy as jnp
from jax import lax
from jax.experimental import pallas as pl
from jax.experimental.pallas import tpu as pltpu
from jax.sharding import PartitionSpec as P

epsilon = 1e-05
MESH = pl.DeviceIdType.MESH
ROWS = 32
LANES = 128


def factor(count):
    small = 1
    for d in range(1, count + 1):
        if count % d == 0 and d * d <= count:
            small = d
    return count // small, small


def chunks_of(F):
    for count in (4, 2):
        if F % (count * LANES) == 0:
            return count
    return 1


def kernel(sizes, hid, gain, w, vg, dx, dw, dgain,
           hv, cols, nm, vgs, vgx, wx, invc, inv_rows, gn, rsc, rs, cenc, cg, wp, wr1, ws1, wr2, gacc, gbuf,
           s_load, s_h, r_h, s_hx, r_hx, s_v, r_v, s_vx, r_vx, s_w, r_w, s_i, r_i,
           s_rs, r_rs, s_b, r_b, s_bx, r_bx, s_p, r_p, s_g, r_g):
    nrep, n, ntp = sizes
    r, f, c = lax.axis_index("rep"), lax.axis_index("fsdp"), lax.axis_index("tp")
    T, D = hid.shape
    F, K = w.shape
    Th = T // ntp
    C = chunks_of(F)
    Fc = F // C
    average = 1.0 / (nrep * n)
    wide = Fc // LANES
    nt = (((1,), (1,)), ((), ()))
    tn = (((0,), (0,)), ((), ()))

    def remote(src, dst, ssem, rsem, dev):
        return pltpu.make_async_remote_copy(src_ref=src, dst_ref=dst, send_sem=ssem, recv_sem=rsem,
                                            device_id=dev, device_id_type=MESH)

    def span(start, count, unit=LANES):
        return pl.ds(pl.multiple_of(start, unit), count)

    def half(j, h):
        return span(j * T + h * Th, Th)

    def full(j):
        return span(j * T, T)

    def tokens(h):
        return span(h * Th, Th)

    def mine(j):
        return span(j * Th, Th)

    def chunk(q):
        return slice(q * Fc, (q + 1) * Fc)

    zpeer = [lax.rem(f + s, n) for s in range(n)]
    zfrom = [lax.rem(f + n - s, n) for s in range(n)]
    tpeer = [lax.rem(c + s, ntp) for s in range(ntp)]
    tfrom = [lax.rem(c + ntp - s, ntp) for s in range(ntp)]
    rpeer = [lax.rem(r + s, nrep) for s in range(nrep)]

    load_h = pltpu.make_async_copy(hid, hv, s_load.at[0])
    load_v = pltpu.make_async_copy(vg, vgs.at[full(f)], s_load.at[1])
    load_w = pltpu.make_async_copy(w, wx.at[c], s_load.at[2])
    load_h.start()
    load_v.start()
    load_w.start()

    barrier = pltpu.get_barrier_semaphore()
    for s in range(1, n):
        pl.semaphore_signal(barrier, inc=1, device_id={"fsdp": zpeer[s]}, device_id_type=MESH)
    for a in range(nrep):
        for b in range(ntp):
            if a or b:
                pl.semaphore_signal(barrier, inc=1, device_id={"rep": rpeer[a], "tp": tpeer[b]}, device_id_type=MESH)
    pl.semaphore_wait(barrier, n - 1 + nrep * ntp - 1)

    def hop_v(d, right):
        j = f - d if right else f + d
        src = vg if d == 0 else vgs.at[full(j)]
        return remote(src, vgs.at[full(j)], s_v.at[int(right), d], r_v.at[j], {"fsdp": f + 1 if right else f - 1})

    def has_v(d, right):
        return f - d >= 0 if right else f + d < n

    def sends_v(d, right):
        return jnp.logical_and(has_v(d, right), f + 1 < n if right else f >= 1)

    def pass_v(j, b, own=False):
        src = vg.at[tokens(tpeer[b])] if own else vgs.at[half(j, tpeer[b])]
        return remote(src, vgx.at[b, mine(j)], s_vx.at[b, j], r_vx.at[b, j], {"tp": tpeer[b]})

    def send_h(q, s):
        columns = span(zpeer[s] * F + q * Fc, Fc)
        return remote(hid.at[tokens(c), columns], cols.at[half(f, c), chunk(q)], s_h.at[q, s], r_h.at[q, s], {"fsdp": zpeer[s]})

    def got_h(q, s):
        ref = cols.at[half(zfrom[s], c), chunk(q)]
        return remote(ref, ref, s_h.at[q, s], r_h.at[q, s], {"fsdp": zpeer[s]})

    def pass_h(q, s, b):
        ref = cols.at[half(zfrom[s], c), chunk(q)]
        return remote(ref, ref, s_hx.at[b, q * n + s], r_hx.at[b, q * n + s], {"tp": tpeer[b]})

    def took_h(q, s, b):
        ref = cols.at[half(zfrom[s], tfrom[b]), chunk(q)]
        return remote(ref, ref, s_hx.at[b, q * n + s], r_hx.at[b, q * n + s], {"tp": tpeer[b]})

    def send_i(s):
        return remote(inv_rows.at[f], inv_rows.at[f], s_i.at[s], r_i.at[s], {"fsdp": zpeer[s]})

    def got_i(s):
        ref = inv_rows.at[zfrom[s]]
        return remote(ref, ref, s_i.at[s], r_i.at[s], {"fsdp": zpeer[s]})

    def pass_w(b):
        return remote(w, wx.at[c], s_w.at[b], r_w.at[b], {"tp": tpeer[b]})

    def took_w(b):
        ref = wx.at[tfrom[b]]
        return remote(ref, ref, s_w.at[b], r_w.at[b], {"tp": tpeer[b]})

    def arrive_v(d):
        for right in (True, False):
            @pl.when(has_v(d, right))
            def _():
                j = f - d if right else f + d
                hop_v(d, right).wait_recv()
                for b in range(1, ntp):
                    pass_v(j, b).start()

            @pl.when(sends_v(d, right))
            def _():
                hop_v(d, right).start()

    for right in (True, False):
        @pl.when(sends_v(0, right))
        def _():
            hop_v(0, right).start()
    for b in range(1, ntp):
        pass_w(b).start()
        pass_v(f, b, True).start()

    load_h.wait()

    @pl.loop(0, T // ROWS)
    def _(i):
        rows = span(i * ROWS, ROWS, ROWS)
        acc = jnp.zeros((ROWS, LANES), jnp.float32)
        for k in range(D // LANES):
            x = hv[rows, k * LANES:(k + 1) * LANES].astype(jnp.float32)
            acc = acc + x * x
        inv = lax.rsqrt(jnp.sum(acc, axis=1, keepdims=True) / D + epsilon)
        invc[span(f * T + i * ROWS, ROWS, ROWS), :] = jnp.broadcast_to(inv, (ROWS, LANES))

    for k in range(T // LANES):
        inv_rows[f, :, k * LANES:(k + 1) * LANES] = invc[span(f * T + k * LANES, LANES), :].T[:8, :]
    for s in range(1, n):
        send_i(s).start()
    order = sorted(range(1, n), key=lambda s: -abs(2 * s - n))
    if n > 1:
        arrive_v(1)
    for s in order:
        send_h(0, s).start()
    for d in range(2, n):
        arrive_v(d)
    for q in range(1, C):
        for s in order:
            send_h(q, s).start()

    cols[full(f), :] = hv[:, span(f * F, F)]
    load_v.wait()
    load_w.wait()
    for j in range(n):
        vgx[0, mine(j), :] = vgs[half(j, c), :]
    for s in range(1, n):
        j = zfrom[s]
        got_i(s).wait_recv()
        for k in range(T // LANES):
            row = inv_rows[j, :1, k * LANES:(k + 1) * LANES]
            invc[span(j * T + k * LANES, LANES), :] = jnp.broadcast_to(row, (LANES, LANES)).T
    gacc[...] = jnp.zeros_like(gacc)
    rsc[...] = jnp.zeros_like(rsc)

    def spread(x, count=wide):
        return jnp.concatenate([x] * count, axis=1) if count > 1 else x

    def arrive_h(q):
        for s in order:
            got_h(q, s).wait_recv()
            for b in range(1, ntp):
                pass_h(q, s, b).start()

    def products(q):
        gains = gain[:, chunk(q)]
        for b in range(ntp):
            part = lax.dot_general(vgx[b], wx[tfrom[b], chunk(q), :], nt, preferred_element_type=jnp.float32)
            gn[:, chunk(q)] = part if b == 0 else gn[:, chunk(q)] + part

        @pl.loop(0, n)
        def _(j):
            @pl.loop(0, Th // ROWS)
            def _(i):
                rows = span(j * T + c * Th + i * ROWS, ROWS, ROWS)
                here = span(j * Th + i * ROWS, ROWS, ROWS)
                t = gn[here, chunk(q)] * (cols[rows, chunk(q)].astype(jnp.float32) * spread(invc[rows, :]))
                gacc[:, chunk(q)] += jnp.sum(t.reshape(ROWS // 8, 8, Fc), axis=0)
                scaled = t * gains
                part = scaled[:, :LANES]
                for k in range(1, wide):
                    part = part + scaled[:, k * LANES:(k + 1) * LANES]
                rsc[here, :] += part

    def partial(q):
        gains = gain[:, chunk(q)]

        @pl.loop(0, n * T // ROWS)
        def _(i):
            rows = span(i * ROWS, ROWS, ROWS)
            normal = cols[rows, chunk(q)].astype(jnp.float32) * spread(invc[rows, :])
            nm[rows, chunk(q)] = (normal * gains).astype(jnp.bfloat16)

        wp[chunk(q), :] = lax.dot_general(nm[:, chunk(q)], vgs[...], tn, preferred_element_type=jnp.float32)

    A, B = factor(nrep)
    ra, rb = r // B, lax.rem(r, B)
    Fh = Fc // 2

    def axes(o):
        first = (rb, B, lambda i: {"rep": ra * B + i})
        second = (ra, A, lambda i: {"rep": i * B + rb})
        return (first, second) if o == 0 else (second, first)

    def rows1(q, o, i):
        size = Fh // axes(o)[0][1]
        return span(q * Fc + o * Fh + i * size, size, 8)

    def rows2(q, o, i):
        size = Fh // nrep
        return span(q * Fc + o * Fh + axes(o)[0][0] * (size * axes(o)[1][1]) + i * size, size, 8)

    def copy_p(stage, q, o, s):
        first, second = axes(o)
        mine_at, count, dev = (first, second, second, first)[stage]
        to = lax.rem(mine_at + s, count)
        if stage == 0:
            src, dst = wp.at[rows1(q, o, to)], wr1.at[q, o, s, :Fh // first[1]]
        elif stage == 1:
            size = Fh // nrep
            src, dst = ws1.at[q, o, span(to * size, size, 8)], wr2.at[q, o, s]
        elif stage == 2:
            src = dst = dw.at[rows2(q, o, mine_at)]
        else:
            src = dst = dw.at[rows1(q, o, mine_at)]
        at = (stage * C + q) * 2 + o
        return remote(src, dst, s_p.at[at, s], r_p.at[at, s], dev(to))

    def got_p(stage, q, o, s):
        first, second = axes(o)
        mine_at, count, dev = (first, second, second, first)[stage]
        source = lax.rem(mine_at + count - s, count)
        at = (stage * C + q) * 2 + o
        if stage == 0:
            ref = wr1.at[q, o, s, :Fh // first[1]]
        elif stage == 1:
            ref = wr2.at[q, o, s]
        elif stage == 2:
            ref = dw.at[rows2(q, o, source)]
        else:
            ref = dw.at[rows1(q, o, source)]
        return remote(ref, ref, s_p.at[at, s], r_p.at[at, s], dev(lax.rem(mine_at + s, count)))

    def counts(stage, o):
        first, second = axes(o)
        return (first, second, second, first)[stage][1]

    def stage_p(stage, q):
        for o in range(2):
            first, second = axes(o)
            if stage:
                for s in range(1, counts(stage - 1, o)):
                    got_p(stage - 1, q, o, s).wait_recv()
            if stage == 1:
                total = wp[rows1(q, o, first[0]), :]
                for s in range(1, first[1]):
                    total = total + wr1[q, o, s, :Fh // first[1]]
                ws1[q, o, :Fh // first[1]] = total
            elif stage == 2:
                size = Fh // nrep
                total = ws1[q, o, span(second[0] * size, size, 8)]
                for s in range(1, second[1]):
                    total = total + wr2[q, o, s]
                dw[rows2(q, o, second[0]), :] = total * average
            if stage < 4:
                for s in range(1, counts(stage, o)):
                    copy_p(stage, q, o, s).start()

    done = [0] * C

    def advance(steps):
        for q, upto in steps:
            while done[q] < upto:
                stage_p(done[q], q)
                done[q] += 1

    def send_rs(s):
        return remote(rs.at[f], rs.at[f], s_rs.at[s], r_rs.at[s], {"fsdp": zpeer[s]})

    def got_rs(s):
        ref = rs.at[zfrom[s]]
        return remote(ref, ref, s_rs.at[s], r_rs.at[s], {"fsdp": zpeer[s]})

    for b in range(1, ntp):
        took_w(b).wait_recv()
        for j in range(n):
            pass_v(j, b).wait_recv()

    for q in range(C):
        arrive_h(q)
        if q == C - 1:
            products(q)
            for j in range(n):
                for k in range(Th // LANES):
                    block = rsc[span(j * Th + k * LANES, LANES), :].T
                    rs[f, j:j + 1, k * LANES:(k + 1) * LANES] = jnp.sum(block, axis=0, keepdims=True)
            for s in range(1, n):
                send_rs(s).start()
        for s in order:
            for b in range(1, ntp):
                took_h(q, s, b).wait_recv()
        partial(q)
        advance([(q, 1)])
        if q < C - 1:
            products(q)
        advance([(p, q - p + 1) for p in range(q)])

    slot = r * ntp + c
    gbuf[slot] = jnp.sum(gacc[...], axis=0, keepdims=True)

    def send_g(a, b):
        return remote(gbuf.at[slot], gbuf.at[slot], s_g.at[a, b], r_g.at[a, b], {"rep": rpeer[a], "tp": tpeer[b]})

    def got_g(a, b):
        ref = gbuf.at[lax.rem(r + nrep - a, nrep) * ntp + tfrom[b]]
        return remote(ref, ref, s_g.at[a, b], r_g.at[a, b], {"rep": rpeer[a], "tp": tpeer[b]})

    others = [(a, b) for a in range(nrep) for b in range(ntp) if a or b]
    for a, b in others:
        send_g(a, b).start()

    for s in range(1, n):
        got_rs(s).wait_recv()
    center = rs[0, :n, :]
    for s in range(1, n):
        center = center + rs[s, :n, :]
    cenc[:n, :] = center / D

    def send_b(s):
        return remote(cg.at[mine(zpeer[s])], dx.at[tokens(c), span(f * F, F)], s_b.at[s], r_b.at[s], {"fsdp": zpeer[s]})

    def got_b(s):
        ref = dx.at[tokens(c), span(zfrom[s] * F, F)]
        return remote(ref, ref, s_b.at[s], r_b.at[s], {"fsdp": zpeer[s]})

    def pass_b(s, b):
        ref = dx.at[tokens(c), span(zfrom[s] * F, F)]
        return remote(ref, ref, s_bx.at[b, s], r_bx.at[b, s], {"tp": tpeer[b]})

    def took_b(s, b):
        ref = dx.at[tokens(tfrom[b]), span(zfrom[s] * F, F)]
        return remote(ref, ref, s_bx.at[b, s], r_bx.at[b, s], {"tp": tpeer[b]})

    for s in [*order, 0]:
        j = zpeer[s]
        for k in range(Th // LANES):
            row = cenc[pl.ds(j, 1), k * LANES:(k + 1) * LANES]
            rsc[k * LANES:(k + 1) * LANES, :] = jnp.broadcast_to(row, (LANES, LANES)).T

        @pl.loop(0, Th // ROWS)
        def _(i):
            rows = span(j * T + c * Th + i * ROWS, ROWS, ROWS)
            here = span(j * Th + i * ROWS, ROWS, ROWS)
            inv, cen = invc[rows, :], rsc[span(i * ROWS, ROWS, ROWS), :]
            for q in range(C):
                scale = spread(inv)
                normal = cols[rows, chunk(q)].astype(jnp.float32) * scale
                cg[here, chunk(q)] = (scale * (gn[here, chunk(q)] * gain[:, chunk(q)] - normal * spread(cen))).astype(jnp.bfloat16)

        if s:
            send_b(s).start()
        else:
            dx[tokens(c), span(f * F, F)] = cg[mine(f), :]
            for b in range(1, ntp):
                pass_b(0, b).start()

    for stage in range(2, 5):
        advance([(q, min(5, max(done[q] + 1, stage))) for q in range(C)])
    for a, b in others:
        got_g(a, b).wait_recv()
    gsum = gbuf[0]
    for i in range(1, nrep * ntp):
        gsum = gsum + gbuf[i]
    dgain[...] = gsum * average

    for s in order:
        got_b(s).wait_recv()
        for b in range(1, ntp):
            pass_b(s, b).start()
    advance([(q, 5) for q in range(C)])
    for s in range(n):
        for b in range(1, ntp):
            took_b(s, b).wait_recv()
    for d in range(n):
        for right in (True, False):
            @pl.when(sends_v(d, right))
            def _():
                hop_v(d, right).wait_send()
    for s in range(1, n):
        for copy in (send_i(s), send_rs(s), send_b(s), *[send_h(q, s) for q in range(C)]):
            copy.wait_send()
    for q in range(C):
        for o in range(2):
            for stage in range(4):
                for s in range(1, counts(stage, o)):
                    copy_p(stage, q, o, s).wait_send()
    for a, b in others:
        send_g(a, b).wait_send()
    for b in range(1, ntp):
        pass_w(b).wait_send()
        for s in range(n):
            pass_v(s, b).wait_send()
            pass_b(s, b).wait_send()
            if s:
                for q in range(C):
                    pass_h(q, s, b).wait_send()


def shards(hidden, norm_gain, value_weight, value_grad):
    nrep, n, ntp = (lax.axis_size(a) for a in ("rep", "fsdp", "tp"))
    T, D = hidden.shape
    F, K = value_weight.shape
    Th = T // ntp
    C = chunks_of(F)
    Fh = F // C // 2
    A, B = factor(nrep)
    G = n * T
    n8 = -(-n // 8) * 8
    dma = pltpu.SemaphoreType.DMA
    f32, bf16 = jnp.float32, jnp.bfloat16
    V = pltpu.VMEM
    vmem = pl.BlockSpec(memory_space=pltpu.VMEM)
    hbm = pl.BlockSpec(memory_space=pl.ANY)
    dx, dw, dgain = pl.pallas_call(
        functools.partial(kernel, (nrep, n, ntp)),
        out_shape=(jax.ShapeDtypeStruct((T, D), bf16), jax.ShapeDtypeStruct((F, K), f32),
                   jax.ShapeDtypeStruct((1, F), f32)),
        in_specs=[hbm, vmem, hbm, hbm],
        out_specs=(vmem, vmem, vmem),
        scratch_shapes=[
            V((T, D), bf16), V((G, F), bf16), V((G, F), bf16), V((G, K), bf16), V((ntp, n * Th, K), bf16),
            V((ntp, F, K), bf16), V((G, LANES), f32), V((n, 8, T), f32), V((n * Th, F), f32), V((n * Th, LANES), f32),
            V((n, n8, Th), f32), V((n8, Th), f32), V((n * Th, F), bf16), V((F, K), f32),
            V((C, 2, A, Fh // B, K), f32), V((C, 2, Fh // B, K), f32), V((C, 2, A, Fh // nrep, K), f32),
            V((8, F), f32), V((nrep * ntp, 1, F), f32),
            dma((3,)), dma((C, n)), dma((C, n)), dma((ntp, C * n)), dma((ntp, C * n)), dma((2, n)), dma((n,)),
            dma((ntp, n)), dma((ntp, n)), dma((ntp,)), dma((ntp,)), dma((n,)), dma((n,)),
            dma((n,)), dma((n,)), dma((n,)), dma((n,)), dma((ntp, n)), dma((ntp, n)),
            dma((8 * C, A)), dma((8 * C, A)), dma((nrep, ntp)), dma((nrep, ntp)),
        ],
        compiler_params=pltpu.CompilerParams(collective_id=0, has_side_effects=True, vmem_limit_bytes=60 * 1024 * 1024),
    )(hidden, norm_gain.reshape(1, F), value_weight, value_grad)
    return dx, dw, dgain.reshape(F)


def solution(mesh):
    placed = (P(("rep", "fsdp"), None), P("fsdp"), P("fsdp", "tp"), P(("rep", "fsdp"), "tp"))
    return jax.shard_map(
        shards,
        mesh=mesh,
        in_specs=placed,
        out_specs=(P(("rep", "fsdp"), None), P("fsdp", "tp"), P("fsdp")),
        check_vma=False,
    )
```

time: 114 us -> 95.6 us (0.84)
  Pallas kernels: 108 us -> 89.6 us
    pallas_call x1, Pallas kernels: 108 us -> 89.6 us  [shards(): pl.pallas_call(functools.partial(kernel, (nrep, n, ntp)), out_shape=(jax....]
where the time goes in v2:
time: 95.6 us; the launch traced here: 95.5 us
  Pallas kernels  89.6 us (94%)
  local copies, waits for them, and re-layouts  5.2 us (5%)
    pallas_call x1, Pallas kernels, shards(): pl.pallas_call(functools.partial(kernel, (nrep, n, ntp)), out_shape=(jax....  89.6 us
    unnamed x7, local copies, waits for them, and re-layouts  5.2 us

profile of v2, /device:TPU:0, one launch (start us, length us, event | category | flops | bytes accessed | tf_op | source)
XLA Modules:
  0.0 95.5 jit_solution(12055764532938449325)
XLA Ops:
  0.6 89.6 %shard_map.67 = (bf16[256,4096]{1,0:T(8,128)(2,1)}, f32[1024,512]{1,0:T(8,128)}, f32[1,1024]{1,0:T(1,128)}) custom-call(bf16[256,4096]{1,0:T(8,128)(2,1)} %hid.1, f32[1,1024]{1,0:T(1,128)} %bitcast.2, bf16[1024,512]{1,0:T(8,128)(2,1)} %w.1, bf16[256,512]{1,0:T(8,128)(2,1)} %vg.1), custom_call_target="tpu_custom_call" | custom-call | tf_op jit(solution)/shard_map/pallas_call | solution.py:466
  90.2 0.0 copy-start
  90.3 3.3 %copy.10 = bf16[256,4096]{1,0:T(8,128)(2,1)} copy(bf16[256,4096]{1,0:T(8,128)(2,1)} %get-tuple-element.12) | data formatting | bytes 4194304
  93.5 0.0 copy-done
  93.5 0.0 copy-start.1
  93.5 1.3 %copy.11 = f32[1024,512]{1,0:T(8,128)} copy(f32[1024,512]{1,0:T(8,128)S(1)} %copy-done) | data formatting | bytes 4194304
  94.9 0.0 copy-done.1
  94.9 0.6 copy.12
Async XLA Ops:
  90.2 3.3 %copy-start = (f32[1024,512]{1,0:T(8,128)S(1)}, f32[1024,512]{1,0:T(8,128)}, u32[]{:S(2)}) copy-start(f32[1024,512]{1,0:T(8,128)} %get-tuple-element.13) | copy-start | bytes 6291460
  93.5 1.3 %copy-start.1 = (f32[1,1024]{1,0:T(1,128)S(1)}, f32[1,1024]{1,0:T(1,128)}, u32[]{:S(2)}) copy-start(f32[1,1024]{1,0:T(1,128)} %get-tuple-element.8) | copy-start | bytes 12292

commit v3 on v2

--- a/solution.py
+++ b/solution.py
@@ -150,6 +150,9 @@
         @pl.when(sends_v(0, right))
         def _():
             hop_v(0, right).start()
+    order = list(range(1, n))
+    for s in order:
+        send_h(0, s).start()
     for b in range(1, ntp):
         pass_w(b).start()
         pass_v(f, b, True).start()
@@ -170,16 +173,12 @@
         inv_rows[f, :, k * LANES:(k + 1) * LANES] = invc[span(f * T + k * LANES, LANES), :].T[:8, :]
     for s in range(1, n):
         send_i(s).start()
-    order = sorted(range(1, n), key=lambda s: -abs(2 * s - n))
-    if n > 1:
-        arrive_v(1)
-    for s in order:
-        send_h(0, s).start()
-    for d in range(2, n):
-        arrive_v(d)
-    for q in range(1, C):
-        for s in order:
-            send_h(q, s).start()
+    for d in range(1, max(n, C)):
+        if d < n:
+            arrive_v(d)
+        if d < C:
+            for s in order:
+                send_h(d, s).start()
 
     cols[full(f), :] = hv[:, span(f * F, F)]
     load_v.wait()
@@ -312,7 +311,7 @@
 
     def advance(steps):
         for q, upto in steps:
-            while done[q] < upto:
+            while done[q] < min(upto, 5):
                 stage_p(done[q], q)
                 done[q] += 1
 
@@ -345,7 +344,7 @@
         advance([(q, 1)])
         if q < C - 1:
             products(q)
-        advance([(p, q - p + 1) for p in range(q)])
+            advance([(p, q - p + 1) for p in range(q)])
 
     slot = r * ntp + c
     gbuf[slot] = jnp.sum(gacc[...], axis=0, keepdims=True)
@@ -406,8 +405,8 @@
             for b in range(1, ntp):
                 pass_b(0, b).start()
 
-    for stage in range(2, 5):
-        advance([(q, min(5, max(done[q] + 1, stage))) for q in range(C)])
+    for stage in range(2, 6):
+        advance([(q, max(done[q] + 1, stage)) for q in range(C)])
     for a, b in others:
         got_g(a, b).wait_recv()
     gsum = gbuf[0]
@@ -448,6 +447,15 @@
                     pass_h(q, s, b).wait_send()
 
 
+def store(*refs):
+    sems = refs[-1]
+    copies = [pltpu.make_async_copy(refs[i], refs[i + 3], sems.at[i]) for i in range(3)]
+    for copy in copies:
+        copy.start()
+    for copy in copies:
+        copy.wait()
+
+
 def shards(hidden, norm_gain, value_weight, value_grad):
     nrep, n, ntp = (lax.axis_size(a) for a in ("rep", "fsdp", "tp"))
     T, D = hidden.shape
@@ -465,8 +473,7 @@
     hbm = pl.BlockSpec(memory_space=pl.ANY)
     dx, dw, dgain = pl.pallas_call(
         functools.partial(kernel, (nrep, n, ntp)),
-        out_shape=(jax.ShapeDtypeStruct((T, D), bf16), jax.ShapeDtypeStruct((F, K), f32),
-                   jax.ShapeDtypeStruct((1, F), f32)),
+        out_shape=(V((T, D), bf16), V((F, K), f32), V((1, F), f32)),
         in_specs=[hbm, vmem, hbm, hbm],
         out_specs=(vmem, vmem, vmem),
         scratch_shapes=[
@@ -480,8 +487,16 @@
             dma((n,)), dma((n,)), dma((n,)), dma((n,)), dma((ntp, n)), dma((ntp, n)),
             dma((8 * C, A)), dma((8 * C, A)), dma((nrep, ntp)), dma((nrep, ntp)),
         ],
-        compiler_params=pltpu.CompilerParams(collective_id=0, has_side_effects=True, vmem_limit_bytes=60 * 1024 * 1024),
+        compiler_params=pltpu.CompilerParams(collective_id=0, has_side_effects=True, vmem_limit_bytes=59 * 1024 * 1024),
     )(hidden, norm_gain.reshape(1, F), value_weight, value_grad)
+    dx, dw, dgain = pl.pallas_call(
+        store,
+        out_shape=tuple(jax.ShapeDtypeStruct(x.shape, x.dtype) for x in (dx, dw, dgain)),
+        in_specs=[vmem] * 3,
+        out_specs=(hbm,) * 3,
+        scratch_shapes=[dma((3,))],
+        compiler_params=pltpu.CompilerParams(vmem_limit_bytes=16 * 1024 * 1024),
+    )(dx, dw, dgain)
     return dx, dw, dgain.reshape(F)
 
 

time: 95.6 us -> 90.6 us (0.948)
  local copies, waits for them, and re-layouts: 5.2 us -> 0 us
    unnamed x7 -> x0, local copies, waits for them, and re-layouts: 5.2 us -> none
    pallas_call x1 -> x2, Pallas kernels: 89.6 us -> 89.8 us  [the longest x1 87.8 us: shards(): pl.pallas_call(functools.partial(kernel, (nrep, n, ntp)), out_shape=(V((T...]
where the time goes in v3:
time: 90.6 us; the launch traced here: 90.5 us
  Pallas kernels  89.8 us (99%)
    pallas_call x1, Pallas kernels, shards(): pl.pallas_call(functools.partial(kernel, (nrep, n, ntp)), out_shape=(V((T...  87.8 us
    pallas_call x1, Pallas kernels, shards(): pl.pallas_call(store, out_shape=tuple((jax.ShapeDtypeStruct(x.shape, x.dt...  2.04 us

profile of v3, /device:TPU:0, one launch (start us, length us, event | category | flops | bytes accessed | tf_op | source)
XLA Modules:
  0.0 90.5 jit_solution(185363630980083011)
XLA Ops:
  0.6 87.8 %shard_map.67 = (bf16[256,4096]{1,0:T(8,128)(2,1)S(1)}, f32[1024,512]{1,0:T(8,128)S(1)}, f32[1,1024]{1,0:T(1,128)S(1)}) custom-call(bf16[256,4096]{1,0:T(8,128)(2,1)} %hid.1, f32[1,1024]{1,0:T(1,128)} %bitcast.2, bf16[1024,512]{1,0:T(8,128)(2,1)} %w.1, bf16[256,512]{1,0:T(8,128)(2,1)} %vg.1), custom_call_target="tpu_custom_call" | custom-call | tf_op jit(solution)/shard_map/pallas_call | solution.py:474
  88.4 2.0 %shard_map.68 = (bf16[256,4096]{1,0:T(8,128)(2,1)}, f32[1024,512]{1,0:T(8,128)}, f32[1,1024]{1,0:T(1,128)}) custom-call(bf16[256,4096]{1,0:T(8,128)(2,1)S(1)} %get-tuple-element.9.refs_0_, f32[1024,512]{1,0:T(8,128)S(1)} %get-tuple-element.10.refs_1_, f32[1,1024]{1,0:T(1,128)S(1)} %get-tuple-element.11.refs_2_), custom_call_target="tpu_custom_call" | custom-call | tf_op jit(solution)/shard_map/pallas_call | solution.py:492

commit v4 on v3

--- a/solution.py
+++ b/solution.py
@@ -88,10 +88,11 @@
                 pl.semaphore_signal(barrier, inc=1, device_id={"rep": rpeer[a], "tp": tpeer[b]}, device_id_type=MESH)
     pl.semaphore_wait(barrier, n - 1 + nrep * ntp - 1)
 
-    def hop_v(d, right):
+    def hop_v(d, right, p):
         j = f - d if right else f + d
-        src = vg if d == 0 else vgs.at[full(j)]
-        return remote(src, vgs.at[full(j)], s_v.at[int(right), d], r_v.at[j], {"fsdp": f + 1 if right else f - 1})
+        rows = span(j * T + p * (T // 2), T // 2)
+        src = vg.at[p * (T // 2):(p + 1) * (T // 2)] if d == 0 else vgs.at[rows]
+        return remote(src, vgs.at[rows], s_v.at[2 * int(right) + p, d], r_v.at[p, j], {"fsdp": f + 1 if right else f - 1})
 
     def has_v(d, right):
         return f - d >= 0 if right else f + d < n
@@ -134,22 +135,25 @@
         return remote(ref, ref, s_w.at[b], r_w.at[b], {"tp": tpeer[b]})
 
     def arrive_v(d):
+        for p in range(2):
+            for right in (True, False):
+                @pl.when(has_v(d, right))
+                def _():
+                    j = f - d if right else f + d
+                    hop_v(d, right, p).wait_recv()
+                    if p == 1:
+                        for b in range(1, ntp):
+                            pass_v(j, b).start()
+
+                @pl.when(sends_v(d, right))
+                def _():
+                    hop_v(d, right, p).start()
+
+    for p in range(2):
         for right in (True, False):
-            @pl.when(has_v(d, right))
+            @pl.when(sends_v(0, right))
             def _():
-                j = f - d if right else f + d
-                hop_v(d, right).wait_recv()
-                for b in range(1, ntp):
-                    pass_v(j, b).start()
-
-            @pl.when(sends_v(d, right))
-            def _():
-                hop_v(d, right).start()
-
-    for right in (True, False):
-        @pl.when(sends_v(0, right))
-        def _():
-            hop_v(0, right).start()
+                hop_v(0, right, p).start()
     order = list(range(1, n))
     for s in order:
         send_h(0, s).start()
@@ -426,7 +430,8 @@
         for right in (True, False):
             @pl.when(sends_v(d, right))
             def _():
-                hop_v(d, right).wait_send()
+                hop_v(d, right, 0).wait_send()
+                hop_v(d, right, 1).wait_send()
     for s in range(1, n):
         for copy in (send_i(s), send_rs(s), send_b(s), *[send_h(q, s) for q in range(C)]):
             copy.wait_send()
@@ -482,7 +487,7 @@
             V((n, n8, Th), f32), V((n8, Th), f32), V((n * Th, F), bf16), V((F, K), f32),
             V((C, 2, A, Fh // B, K), f32), V((C, 2, Fh // B, K), f32), V((C, 2, A, Fh // nrep, K), f32),
             V((8, F), f32), V((nrep * ntp, 1, F), f32),
-            dma((3,)), dma((C, n)), dma((C, n)), dma((ntp, C * n)), dma((ntp, C * n)), dma((2, n)), dma((n,)),
+            dma((3,)), dma((C, n)), dma((C, n)), dma((ntp, C * n)), dma((ntp, C * n)), dma((4, n)), dma((2, n)),
             dma((ntp, n)), dma((ntp, n)), dma((ntp,)), dma((ntp,)), dma((n,)), dma((n,)),
             dma((n,)), dma((n,)), dma((n,)), dma((n,)), dma((ntp, n)), dma((ntp, n)),
             dma((8 * C, A)), dma((8 * C, A)), dma((nrep, ntp)), dma((nrep, ntp)),

time: 90.6 us -> 87.6 us (0.967)
  Pallas kernels: 89.8 us -> 86.8 us
    pallas_call x1, Pallas kernels: 87.8 us -> 84.7 us  [shards(): pl.pallas_call(functools.partial(kernel, (nrep, n, ntp)), out_shape=(V((T...]
where the time goes in v4:
time: 87.6 us; the launch traced here: 87.4 us
  Pallas kernels  86.8 us (99%)
    pallas_call x1, Pallas kernels, shards(): pl.pallas_call(functools.partial(kernel, (nrep, n, ntp)), out_shape=(V((T...  84.7 us
    pallas_call x1, Pallas kernels, shards(): pl.pallas_call(store, out_shape=tuple((jax.ShapeDtypeStruct(x.shape, x.dt...  2.04 us

profile of v4, /device:TPU:0, one launch (start us, length us, event | category | flops | bytes accessed | tf_op | source)
XLA Modules:
  0.0 87.4 jit_solution(2533929741668627300)
XLA Ops:
  0.6 84.7 %shard_map.67 = (bf16[256,4096]{1,0:T(8,128)(2,1)S(1)}, f32[1024,512]{1,0:T(8,128)S(1)}, f32[1,1024]{1,0:T(1,128)S(1)}) custom-call(bf16[256,4096]{1,0:T(8,128)(2,1)} %hid.1, f32[1,1024]{1,0:T(1,128)} %bitcast.2, bf16[1024,512]{1,0:T(8,128)(2,1)} %w.1, bf16[256,512]{1,0:T(8,128)(2,1)} %vg.1), custom_call_target="tpu_custom_call" | custom-call | tf_op jit(solution)/shard_map/pallas_call | solution.py:479
  85.4 2.0 %shard_map.68 = (bf16[256,4096]{1,0:T(8,128)(2,1)}, f32[1024,512]{1,0:T(8,128)}, f32[1,1024]{1,0:T(1,128)}) custom-call(bf16[256,4096]{1,0:T(8,128)(2,1)S(1)} %get-tuple-element.9.refs_0_, f32[1024,512]{1,0:T(8,128)S(1)} %get-tuple-element.10.refs_1_, f32[1,1024]{1,0:T(1,128)S(1)} %get-tuple-element.11.refs_2_), custom_call_target="tpu_custom_call" | custom-call | tf_op jit(solution)/shard_map/pallas_call | solution.py:497
